TPU v7x, 32 devices: a whole 2x2x4 slice. The times are simulated.
32 devices in a mesh: gx: 4 (over y, x), gy: 4 (over z), gz: 2 (over core).
Axes of the slice: x: 2, y: 2, z: 4, core: 2. Of those that a mesh axis runs over, the one named last changes fastest.
Arguments:
- rhs: bfloat16 [2, 4096, 4096], P('gz', 'gx', 'gy'), may hold values from -40 to 40
- basis_x: bfloat16 [4096, 4096], P('gx', ('gy', 'gz')), may hold values from -0.125 to 0.125
- basis_y: bfloat16 [4096, 4096], P('gy', ('gx', 'gz')), may hold values from -0.125 to 0.125
- eig_x: float32 [4096], P('gx'), may hold values from 0.1 to 4
- eig_y: float32 [4096], P('gy'), may hold values from 0.1 to 4
- eig_z: float32 [2], P('gz'), may hold values from 0.1 to 4
Outputs:
- solution: bfloat16 [2, 4096, 4096], P('gz', 'gx', 'gy')
- energy: float32 [], replicated
All inputs are finite; a program needn't handle non-finite values.
Results may differ from a plain program's by a relative error of at most 0.01.
Values may be sent and summed in bfloat16 or wider, within the bound.
A program may use at most 128 MiB of HBM per device.

v0:
```python
import functools

import jax
import jax.numpy as jnp
from jax import lax
from jax.experimental import pallas as pl
from jax.experimental.pallas import tpu as pltpu
from jax.sharding import PartitionSpec as P

BF16, F32 = jnp.bfloat16, jnp.float32
LANES = 128


def contract(left, right, dims):
    return lax.dot_general(left, right, ((dims[:1], dims[1:]), ((), ())), preferred_element_type=F32)


def kernel(
    nx, ny, yq,
    rhs, bx, by, ex, ey, ez,
    out, energy,
    bxb, byb, wide, gs, grecv, gall, wbuf, vrecv, vfull, sown, srecv,
    exall, eyall, ezall, dcol, eacc, e1, e2, e3,
    s_loc, s_eig, r_eig, s_head, r_head, s_bxz, r_bxz, s_bxd, r_bxd, s_byz, r_byz, s_byp, r_byp,
    s_g, r_g, s_ga, r_ga, s_gd, r_gd, s_vd, r_vd, s_va, r_va, s_vb, r_vb, s_s, r_s, s_out, s_e, r_e,
):
    p, z, c = lax.axis_index("gx"), lax.axis_index("gy"), lax.axis_index("gz")
    px, py = p % 2, p // 2
    nb = nx // 2
    xb, yb = rhs.shape[1], rhs.shape[2]
    cx, cy = bx.shape[1], by.shape[1]
    ci = cx // 2
    ib = ci // nb
    chunks = yb // yq
    half = yb // 2
    other = 1 - c

    def remote(src, dst, ss, rs, **where):
        return pltpu.make_async_remote_copy(
            src_ref=src, dst_ref=dst, send_sem=ss, recv_sem=rs,
            device_id=where, device_id_type=pl.DeviceIdType.MESH,
        )

    def loop(count, body):
        lax.fori_loop(0, count, lambda i, carry: (body(i), carry)[1], 0)

    def cols(start, size):
        return pl.ds(pl.multiple_of(start, LANES), size)

    def rows(start, size):
        return pl.ds(pl.multiple_of(start, size), size)

    barrier = pltpu.get_barrier_semaphore()
    for t in range(1, nx):
        pl.semaphore_signal(barrier, inc=1, device_id={"gx": p ^ t}, device_id_type=pl.DeviceIdType.MESH)
    for d in range(1, ny):
        pl.semaphore_signal(barrier, inc=1, device_id={"gy": (z + d) % ny}, device_id_type=pl.DeviceIdType.MESH)
    pl.semaphore_signal(barrier, inc=1, device_id={"gz": other}, device_id_type=pl.DeviceIdType.MESH)

    mine = rows(px * xb, xb)
    theirs = rows((1 - px) * xb, xb)
    local = [
        pltpu.make_async_copy(by, byb.at[z, p], s_loc.at[0]),
        pltpu.make_async_copy(rhs.at[0], wide.at[mine, :], s_loc.at[1]),
        pltpu.make_async_copy(bx.at[:, cols(px * ci, ci)], bxb.at[z, c, mine, :], s_loc.at[2]),
        pltpu.make_async_copy(ex, exall.at[p], s_loc.at[3]),
        pltpu.make_async_copy(ey, eyall.at[z], s_loc.at[4]),
        pltpu.make_async_copy(ez, ezall.at[c], s_loc.at[5]),
    ]
    for copy in local:
        copy.start()
    pl.semaphore_wait(barrier, nx + ny - 1)

    swap_bx = remote(bx.at[:, cols((1 - px) * ci, ci)], bxb.at[z, c, mine, :], s_head.at[0], r_head.at[0], gx=p ^ 1)
    swap_bx.start()
    for copy in local:
        copy.wait()
    eigs = [remote(exall.at[p], exall.at[p], s_eig.at[t], r_eig.at[t], gx=p ^ t) for t in range(1, nx)]
    eigs += [
        remote(eyall.at[z], eyall.at[z], s_eig.at[nx + d], r_eig.at[nx + d], gy=(z + d) % ny) for d in range(1, ny)
    ]
    eigs += [remote(ezall.at[c], ezall.at[c], s_eig.at[0], r_eig.at[0], gz=other)]
    for copy in eigs:
        copy.start()
    swap_rhs = remote(wide.at[mine, :], wide.at[mine, :], s_head.at[1], r_head.at[1], gx=p ^ 1)

    def line(buffer, ss, rs, zs, up, index):
        ref = buffer.at[(zs,) + index]
        return remote(ref, ref, ss.at[zs, 0 if up else 1], rs.at[zs], gy=jnp.clip(z + (1 if up else -1), 0, ny - 1))

    def bx_line(zs, up):
        return line(bxb, s_bxz, r_bxz, zs, up, (c,))

    def by_line(zs, up):
        return line(byb, s_byz, r_byz, zs, up, (p,))

    def goes_on(up):
        return z + 1 < ny if up else z > 0

    def source(r, up):
        zs = z - r if up else z + r
        return zs, jnp.logical_and(zs >= 0, zs < ny)

    def bx_pass(zs):
        return remote(bxb.at[zs, c], bxb.at[zs, c], s_bxd.at[zs], r_bxd.at[zs], gz=other)

    def piece(zs, owner, part):
        return byb.at[zs, owner, pl.ds(part * half, half), :]

    def plane_copies(zs):
        direct, relay = [], []
        slot = 0
        for b in range(nb):
            t = 2 * b if b else 1
            for part in (0, 1) if t == 1 else (1, 0):
                ref = piece(zs, p, part)
                direct.append(remote(ref, ref, s_byp.at[zs, slot], r_byp.at[zs, t, part], gx=p ^ t))
                slot += 1
        for b in range(1, nb):
            ref = piece(zs, p ^ 1, 0)
            relay.append(((1, 0), remote(ref, ref, s_byp.at[zs, slot], r_byp.at[zs, 2 * b + 1, 0], gx=p ^ (2 * b))))
            slot += 1
        for b in range(1, nb):
            ref = piece(zs, p ^ (2 * b), 1)
            relay.append(((2 * b, 1), remote(ref, ref, s_byp.at[zs, slot], r_byp.at[zs, 2 * b + 1, 1], gx=p ^ 1)))
            slot += 1
        return direct, relay

    def wait_piece(zs, t, part):
        ref = piece(zs, p ^ t, part)
        remote(ref, ref, s_byp.at[zs, 0], r_byp.at[zs, t, part], gx=p ^ 1).wait_recv()

    def relays(zs):
        seen = set()
        for key, copy in plane_copies(zs)[1]:
            if key not in seen:
                seen.add(key)
                wait_piece(zs, *key)
            copy.start()

    def g_copies(zs):
        return [
            remote(gs.at[zs, py ^ b], grecv.at[zs, b - 1], s_g.at[zs, b - 1], r_g.at[zs, b - 1], gx=p ^ (2 * b))
            for b in range(1, nb)
        ]

    def first(zs):
        bx_pass_in(zs).wait_recv()

        def tile(i):
            cc, n = i // (yb // yq), i % (yb // yq)
            part = contract(bxb[zs, cc], wide[:, cols(n * yq, yq)], (0, 0)).astype(BF16)
            for b in range(nb):
                gs[zs, b, cc, :, cols(n * yq, yq)] = part[b * ib : (b + 1) * ib]

        loop(2 * (yb // yq), tile)
        for copy in g_copies(zs):
            copy.start()

    def bx_pass_in(zs):
        return remote(bxb.at[zs, other], bxb.at[zs, other], s_bxd.at[zs], r_bxd.at[zs], gz=other)

    def g_send(zs):
        return remote(gs.at[zs, py], gall.at[z, c], s_ga.at[zs], r_ga.at[z], gy=zs)

    def g_pass(zs, core):
        return remote(gall.at[zs, core], gall.at[zs, core], s_gd.at[zs], r_gd.at[zs], gz=other)

    def collect(zs):
        for copy in g_copies(zs):
            copy.wait_recv()

        def tile(i):
            cc, n = i // (yb // yq), i % (yb // yq)
            lanes = cols(n * yq, yq)
            total = gs[zs, py, cc, :, lanes].astype(F32)
            for b in range(1, nb):
                total = total + grecv[zs, b - 1, cc, :, lanes].astype(F32)

            @pl.when(zs != z)
            def _():
                gs[zs, py, cc, :, lanes] = total.astype(BF16)

            @pl.when(zs == z)
            def _():
                gall[z, c, cc, :, lanes] = total.astype(BF16)

        loop(2 * (yb // yq), tile)

        @pl.when(zs != z)
        def _():
            g_send(zs).start()

        @pl.when(zs == z)
        def _():
            g_pass(z, c).start()

    def start_line(maker, zs, r):
        for up in (True, False):
            @pl.when(goes_on(up))
            def _(up=up):
                maker(zs, up).start()

    def start_plane(zs):
        for copy in plane_copies(zs)[0]:
            copy.start()

    start_line(by_line, z, 0)
    swap_rhs.start()
    start_plane(z)
    remote(bx.at[:, cols(px * ci, ci)], bxb.at[z, c, theirs, :], s_head.at[0], r_head.at[0], gx=p ^ 1).wait_recv()
    start_line(bx_line, z, 0)
    bx_pass(z).start()

    def forward(maker, r, then):
        for up in (True, False):
            zs, valid = source(r, up)

            @pl.when(valid)
            def _(zs=zs, up=up):
                maker(zs, up).wait_recv()

                @pl.when(goes_on(up))
                def _():
                    maker(zs, up).start()

                then(zs)

    def each(r, act):
        for up in (True, False):
            zs, valid = source(r, up)
            valid = jnp.logical_and(valid, r >= 0)
            if not up:
                valid = jnp.logical_and(valid, r > 0)

            @pl.when(valid)
            def _(zs=zs):
                act(zs)

    def round_of(i):
        r = i + 1
        forward(bx_line, r, lambda zs: bx_pass(zs).start())

        @pl.when(r == 1)
        def _():
            remote(wide.at[theirs, :], wide.at[theirs, :], s_head.at[1], r_head.at[1], gx=p ^ 1).wait_recv()

        each(r - 1, first)
        each(r - 2, relays)
        each(r - 2, collect)
        forward(by_line, r, start_plane)

    loop(ny + 1, round_of)

    for t in range(1, nx):
        remote(exall.at[p ^ t], exall.at[p ^ t], s_eig.at[t], r_eig.at[t], gx=p ^ t).wait_recv()
    for d in range(1, ny):
        far = (z - d) % ny
        remote(eyall.at[far], eyall.at[far], s_eig.at[nx + d], r_eig.at[nx + d], gy=(z + d) % ny).wait_recv()
    remote(ezall.at[other], ezall.at[other], s_eig.at[0], r_eig.at[0], gz=other).wait_recv()
    for cc in range(2):
        start = (z * 2 + cc) * cx + px * ci + py * ib
        line_at = start // LANES
        per = xb // LANES
        row = exall[line_at // per, pl.ds(line_at % per, 1), :]
        lane = lax.broadcasted_iota(jnp.int32, (ib, LANES), 1)
        want = lax.broadcasted_iota(jnp.int32, (ib, LANES), 0) + start % LANES
        column = jnp.sum(jnp.where(lane == want, jnp.broadcast_to(row, (ib, LANES)), 0.0), axis=1, keepdims=True)
        for k in range(2):
            dcol[pl.ds((k * 2 + cc) * ib, ib), :] = jnp.broadcast_to(column, (ib, LANES)) + ezall[k, 0:1, :]

    def arrive(d):
        zs = (z + 1 + d) % ny
        remote(gall.at[zs, c], gall.at[zs, c], s_ga.at[zs], r_ga.at[zs], gy=zs).wait_recv()
        g_pass(zs, c).start()

    loop(ny - 1, arrive)

    def passed(zs):
        g_pass(zs, other).wait_recv()

    loop(ny, passed)
    eacc[...] = jnp.zeros_like(eacc)

    tn = min(cy, 256)

    def second(t):
        owner = p ^ t

        def landed(zs):
            @pl.when(t % 2 == 1)
            def _():
                wait_piece(zs, t, 1)

            @pl.when(t > 1)
            def _():
                wait_piece(zs, t, 0)

        loop(ny, landed)

        def tile(n):
            h = None
            for zs in range(ny):
                term = contract(gall[zs].reshape(4 * ib, yb), byb[zs, owner, :, cols(n * tn, tn)], (1, 0))
                h = term if h is None else h + term
            for l in range(tn // LANES):
                line_at = ((owner * 2 + c) * cy + n * tn) // LANES + l
                per = yb // LANES
                row = eyall[line_at // per, pl.ds(line_at % per, 1), :]
                part = h[:, l * LANES : (l + 1) * LANES]
                w = part / (dcol[...] + row)
                eacc[...] += jnp.sum((part * w).reshape(-1, 8, LANES), axis=0)
                wbuf[owner, :, cols(n * tn + l * LANES, LANES)] = w.astype(BF16)

        loop(cy // tn, tile)

    loop(nx, second)

    def v_pass(q, zs, core):
        lanes = cols(q * yq, yq)
        return remote(gall.at[zs, core, :, :, lanes], vrecv.at[zs, :, :, lanes], s_vd.at[q, zs], r_vd.at[q, zs], gz=other)

    def v_slot(q, zs, owner):
        return vfull.at[q, zs, :, pl.ds(pl.multiple_of(owner * ib, ib), ib), :]

    def v_send(q, zs):
        return remote(
            gall.at[zs, c, :, :, cols(q * yq, yq)], v_slot(q, z, py), s_va.at[q, zs], r_va.at[q, z], gy=zs
        )

    def v_copies(q, zs):
        return [
            remote(v_slot(q, zs, py), v_slot(q, zs, py), s_vb.at[q, zs, b - 1], r_vb.at[q, zs, b - 1], gx=p ^ (2 * b))
            for b in range(1, nb)
        ]

    def third(q):
        def target(d):
            zs = (z + 1 + d) % ny
            v = None
            for owner in range(nx):
                term = contract(wbuf[owner], byb[zs, owner, rows(q * yq, yq), :], (1, 1))
                v = term if v is None else v + term
            gall[zs, :, :, :, cols(q * yq, yq)] = v.astype(BF16).reshape(2, 2, ib, yq)
            v_pass(q, zs, other).start()

        loop(ny, target)

    def merge(q):
        def target(d):
            zs = (z + 1 + d) % ny
            lanes = cols(q * yq, yq)
            v_pass(q, zs, c).wait_recv()
            v = (gall[zs, c, :, :, lanes].astype(F32) + vrecv[zs, :, :, lanes].astype(F32)).astype(BF16)

            @pl.when(zs != z)
            def _():
                gall[zs, c, :, :, lanes] = v
                v_send(q, zs).start()

            @pl.when(zs == z)
            def _():
                vfull[q, zs, :, pl.ds(pl.multiple_of(py * ib, ib), ib), :] = v

        loop(ny, target)

    def spread(q):
        def target(d):
            zs = (z + d) % ny

            @pl.when(zs != z)
            def _():
                remote(v_slot(q, zs, py), v_slot(q, zs, py), s_va.at[q, zs], r_va.at[q, zs], gy=zs).wait_recv()

            for copy in v_copies(q, zs):
                copy.start()

        loop(ny, target)

    mt = min(xb, 512)

    def s_copy(q):
        lanes = cols(q * yq, yq)
        return remote(wide.at[theirs, lanes], srecv.at[:, lanes], s_s.at[q], r_s.at[q], gx=p ^ 1)

    def fourth(q):
        lanes = cols(q * yq, yq)

        def landed(zs):
            for b in range(1, nb):
                slot = v_slot(q, zs, py ^ b)
                remote(slot, slot, s_vb.at[q, zs, b - 1], r_vb.at[q, zs, b - 1], gx=p ^ (2 * b)).wait_recv()

        loop(ny, landed)

        def tile(i):
            m, own = i % (xb // mt), i // (xb // mt)
            side = jnp.where(own == 1, px, 1 - px)
            at = rows(side * xb + m * mt, mt)
            s = None
            for zs in range(ny):
                for cc in range(2):
                    term = contract(bxb[zs, cc, at, :], vfull[q, zs, cc], (1, 0))
                    s = term if s is None else s + term

            @pl.when(own == 0)
            def _():
                wide[at, lanes] = s.astype(BF16)

                @pl.when(m == xb // mt - 1)
                def _():
                    s_copy(q).start()

            @pl.when(own == 1)
            def _():
                sown[rows(m * mt, mt), lanes] = s

        loop(2 * (xb // mt), tile)

    def out_copy(q):
        lanes = cols(q * yq, yq)
        return pltpu.make_async_copy(wide.at[mine, lanes], out.at[0, :, lanes], s_out.at[q])

    def finish(q):
        lanes = cols(q * yq, yq)
        s_copy(q).wait_recv()

        def tile(m):
            at = rows(m * mt, mt)
            wide[rows(px * xb + m * mt, mt), lanes] = (sown[at, lanes] + srecv[at, lanes].astype(F32)).astype(BF16)

        loop(xb // mt, tile)
        out_copy(q).start()

    def left(zs):
        g_pass(zs, c).wait_send()

    loop(ny, left)
    swap_rhs.wait_send()

    e_core = remote(eacc, e1, s_e.at[0], r_e.at[0], gz=other)
    e_plane = [remote(e2.at[p], e2.at[p], s_e.at[t], r_e.at[t], gx=p ^ t) for t in range(1, nx)]
    e_line = [remote(e3.at[z], e3.at[z], s_e.at[nx + d], r_e.at[nx + d], gy=(z + d) % ny) for d in range(1, ny)]

    def leave(t):
        @pl.when(t == 0)
        def _():
            e_core.start()

        @pl.when(t == 1)
        def _():
            e_core.wait_recv()
            e2[p] = eacc[...] + e1[...]
            for copy in e_plane:
                copy.start()

        @pl.when(t == 2)
        def _():
            for s in range(1, nx):
                remote(e2.at[p ^ s], e2.at[p ^ s], s_e.at[s], r_e.at[s], gx=p ^ s).wait_recv()
            total = e2[0]
            for s in range(1, nx):
                total = total + e2[s]
            e3[z] = total
            for copy in e_line:
                copy.start()

        @pl.when(t < chunks)
        def _():
            third(t)

        @pl.when(jnp.logical_and(t >= 1, t <= chunks))
        def _():
            merge(t - 1)

    loop(max(chunks + 1, 3), leave)

    def come(t):
        @pl.when(t < chunks)
        def _():
            spread(t)

        @pl.when(jnp.logical_and(t >= 1, t <= chunks))
        def _():
            fourth(t - 1)

        @pl.when(t >= 2)
        def _():
            finish(t - 2)

    loop(chunks + 2, come)

    for d in range(1, ny):
        far = (z - d) % ny
        remote(e3.at[far], e3.at[far], s_e.at[nx + d], r_e.at[nx + d], gy=(z + d) % ny).wait_recv()
    total = e3[0]
    for s in range(1, ny):
        total = total + e3[s]
    energy[...] = jnp.broadcast_to(jnp.sum(jnp.sum(total, axis=0, keepdims=True), axis=1, keepdims=True), energy.shape)

    swap_bx.wait_send()
    for copy in eigs + [e_core] + e_plane + e_line:
        copy.wait_send()

    def drain(zs):
        for up in (True, False):
            from_here = zs <= z if up else zs >= z

            @pl.when(jnp.logical_and(goes_on(up), from_here))
            def _(up=up):
                bx_line(zs, up).wait_send()
                by_line(zs, up).wait_send()

        bx_pass(zs).wait_send()
        direct, relay = plane_copies(zs)
        for copy in direct + [copy for _, copy in relay] + g_copies(zs):
            copy.wait_send()

        @pl.when(zs != z)
        def _():
            g_send(zs).wait_send()

        def chunk(q):
            v_pass(q, zs, other).wait_send()
            for copy in v_copies(q, zs):
                copy.wait_send()

            @pl.when(zs != z)
            def _():
                v_send(q, zs).wait_send()

        loop(chunks, chunk)

    loop(ny, drain)

    def drain_chunk(q):
        s_copy(q).wait_send()
        out_copy(q).wait()

    loop(chunks, drain_chunk)


def shards(nx, ny, rhs, basis_x, basis_y, eig_x, eig_y, eig_z):
    xb, yb = rhs.shape[1], rhs.shape[2]
    cx, cy = basis_x.shape[1], basis_y.shape[1]
    nb, ci = nx // 2, cx // 2
    ib = ci // nb
    yq = min(yb, 256)
    chunks = yb // yq
    ex = eig_x.reshape(xb // LANES, LANES)
    ey = eig_y.reshape(yb // LANES, LANES)
    ez = jnp.broadcast_to(eig_z.reshape(1, 1), (8, LANES))
    dma = pltpu.SemaphoreType.DMA
    any_space, vmem = pl.BlockSpec(memory_space=pl.ANY), pl.BlockSpec(memory_space=pltpu.VMEM)
    solution, energy = pl.pallas_call(
        functools.partial(kernel, nx, ny, yq),
        name="solve",
        out_shape=(
            jax.ShapeDtypeStruct(rhs.shape, BF16),
            jax.ShapeDtypeStruct((8, LANES), F32),
        ),
        in_specs=[any_space] * 3 + [vmem] * 3,
        out_specs=(any_space, vmem),
        scratch_shapes=[
            pltpu.VMEM((ny, 2, 2 * xb, ci), BF16),
            pltpu.VMEM((ny, nx, yb, cy), BF16),
            pltpu.VMEM((2 * xb, yb), BF16),
            pltpu.VMEM((ny, nb, 2, ib, yb), BF16),
            pltpu.VMEM((ny, nb - 1, 2, ib, yb), BF16),
            pltpu.VMEM((ny, 2, 2, ib, yb), BF16),
            pltpu.VMEM((nx, 4 * ib, cy), BF16),
            pltpu.VMEM((ny, 2, ib, yb), BF16),
            pltpu.VMEM((chunks, ny, 2, nb * ib, yq), BF16),
            pltpu.VMEM((xb, yb), F32),
            pltpu.VMEM((xb, yb), BF16),
            pltpu.VMEM((nx, xb // LANES, LANES), F32),
            pltpu.VMEM((ny, yb // LANES, LANES), F32),
            pltpu.VMEM((2, 8, LANES), F32),
            pltpu.VMEM((4 * ib, LANES), F32),
            pltpu.VMEM((8, LANES), F32),
            pltpu.VMEM((8, LANES), F32),
            pltpu.VMEM((nx, 8, LANES), F32),
            pltpu.VMEM((ny, 8, LANES), F32),
            dma((6,)),
            dma((nx + ny,)), dma((nx + ny,)),
            dma((2,)), dma((2,)),
            dma((ny, 2)), dma((ny,)),
            dma((ny,)), dma((ny,)),
            dma((ny, 2)), dma((ny,)),
            dma((ny, 4 * nb - 2)), dma((ny, nx, 2)),
            dma((ny, nb - 1)), dma((ny, nb - 1)),
            dma((ny,)), dma((ny,)),
            dma((ny,)), dma((ny,)),
            dma((chunks, ny)), dma((chunks, ny)),
            dma((chunks, ny)), dma((chunks, ny)),
            dma((chunks, ny, nb - 1)), dma((chunks, ny, nb - 1)),
            dma((chunks,)), dma((chunks,)),
            dma((chunks,)),
            dma((nx + ny,)), dma((nx + ny,)),
        ],
        compiler_params=pltpu.CompilerParams(
            collective_id=0, has_side_effects=True, vmem_limit_bytes=65472 * 1024
        ),
    )(rhs, basis_x, basis_y, ex, ey, ez)
    return solution, energy[0, 0]


def solution(mesh):
    return jax.shard_map(
        functools.partial(shards, mesh.shape["gx"], mesh.shape["gy"]),
        mesh=mesh,
        in_specs=(
            P("gz", "gx", "gy"),
            P("gx", ("gy", "gz")),
            P("gy", ("gx", "gz")),
            P("gx"),
            P("gy"),
            P("gz"),
        ),
        out_specs=(P("gz", "gx", "gy"), P()),
        check_vma=False,
    )
```

profile of v0, /device:TPU:0, one launch (start us, length us, event | category | flops | bytes accessed | tf_op | source)
XLA Modules:
  0.0 316.3 jit_solution(18372321379444809141)
XLA Ops:
  1.3 0.6 broadcast_in_dim.8.ez
  1.9 310.2 %solve.1 = (bf16[1,1024,1024]{2,1,0:T(8,128)(2,1)}, f32[8,128]{1,0:T(8,128)}) custom-call(bf16[1,1024,1024]{2,1,0:T(8,128)(2,1)} %rhs.1, bf16[1024,512]{1,0:T(8,128)(2,1)} %bx.1, bf16[1024,512]{1,0:T(8,128)(2,1)} %by.1, f32[8,128]{1,0:T(8,128)} %bitcast.5, f32[8,128]{1,0:T(8,128)} %bitcast.6, f32[8,128]{1,0:T(8,128)} %broadcast_in_dim.8.ez), custom_call_target="tpu_custom_call" | custom-call | tf_op jit(solution)/shard_map/solve/pallas_call | solution.py:555
  312.1 1.2 slice.3
  313.2 3.1 copy.10
where the time goes:
time: 322 us; the launch traced here: 316 us
  Pallas kernels  310 us (96%)
  local copies, waits for them, and re-layouts  4.86 us (2%)
    pallas_call x1, Pallas kernels, shards(): pl.pallas_call(functools.partial(kernel, nx, ny, yq), name='solve', out_s...  310 us

commit v1 on v0

v1 whole, which is shorter than its diff:
```python
import functools

import jax
import jax.numpy as jnp
from jax import lax
from jax.experimental import pallas as pl
from jax.experimental.pallas import tpu as pltpu
from jax.sharding import PartitionSpec as P

BF16, F32 = jnp.bfloat16, jnp.float32
LANES = 128


def contract(left, right, dims):
    return lax.dot_general(left, right, ((dims[:1], dims[1:]), ((), ())), preferred_element_type=F32)


def kernel(
    nx, ny, yq,
    rhs, bx, by, ex, ey, ez,
    out, energy,
    bxb, byb, wide, gs, grecv, gall, wbuf, vrecv, vfull, sown, srecv,
    exall, eyall, ezall, dcol, eacc, e1, e2, e3,
    s_loc, s_eig, r_eig, s_head, r_head, s_bxz, r_bxz, s_bxd, r_bxd, s_byf, r_byf, s_byc, r_byc, s_byp, r_byp,
    s_g, r_g, s_ga, r_ga, s_gd, r_gd, s_vd, r_vd, s_va, r_va, s_vb, r_vb, s_s, r_s, s_out, s_e, r_e,
):
    p, z, c = lax.axis_index("gx"), lax.axis_index("gy"), lax.axis_index("gz")
    px, py = p % 2, p // 2
    nb = nx // 2
    xb, yb = rhs.shape[1], rhs.shape[2]
    cx, cy = bx.shape[1], by.shape[1]
    ci = cx // 2
    ib = ci // nb
    chunks = yb // yq
    half = yb // 2
    other = 1 - c
    mid = ny // 2
    low = z < mid
    works = jnp.logical_or(z == mid - 1, z == mid)
    rests = jnp.logical_not(works)
    place = jnp.where(low, 0, 1)

    def when(condition, act):
        @pl.when(condition)
        def _():
            act()

    def remote(src, dst, ss, rs, **where):
        return pltpu.make_async_remote_copy(
            src_ref=src, dst_ref=dst, send_sem=ss, recv_sem=rs,
            device_id=where, device_id_type=pl.DeviceIdType.MESH,
        )

    def loop(count, body):
        lax.fori_loop(0, count, lambda i, carry: (body(i), carry)[1], 0)

    def cols(start, size):
        return pl.ds(pl.multiple_of(start, LANES), size)

    def rows(start, size):
        return pl.ds(pl.multiple_of(start, size), size)

    barrier = pltpu.get_barrier_semaphore()
    for t in range(1, nx):
        pl.semaphore_signal(barrier, inc=1, device_id={"gx": p ^ t}, device_id_type=pl.DeviceIdType.MESH)
    for d in range(1, ny):
        pl.semaphore_signal(barrier, inc=1, device_id={"gy": (z + d) % ny}, device_id_type=pl.DeviceIdType.MESH)
    pl.semaphore_signal(barrier, inc=1, device_id={"gz": other}, device_id_type=pl.DeviceIdType.MESH)

    mine = rows(px * xb, xb)
    theirs = rows((1 - px) * xb, xb)
    local = [
        pltpu.make_async_copy(by, byb.at[z, p], s_loc.at[0]),
        pltpu.make_async_copy(rhs.at[0], wide.at[mine, :], s_loc.at[1]),
        pltpu.make_async_copy(bx.at[:, cols(px * ci, ci)], bxb.at[z, c, mine, :], s_loc.at[2]),
        pltpu.make_async_copy(ex, exall.at[p], s_loc.at[3]),
        pltpu.make_async_copy(ey, eyall.at[z], s_loc.at[4]),
    ]
    for copy in local:
        copy.start()
    pl.semaphore_wait(barrier, nx + ny - 1)

    swap_bx = remote(bx.at[:, cols((1 - px) * ci, ci)], bxb.at[z, c, mine, :], s_head.at[0], r_head.at[0], gx=p ^ 1)
    swap_bx.start()
    swap_rhs = remote(wide.at[mine, :], wide.at[mine, :], s_head.at[1], r_head.at[1], gx=p ^ 1)
    eigs = [remote(exall.at[p], exall.at[p], s_eig.at[t], r_eig.at[t], gx=p ^ t) for t in range(1, nx)]
    eigs += [
        remote(eyall.at[z], eyall.at[z], s_eig.at[nx + d], r_eig.at[nx + d], gy=(z + d) % ny) for d in range(1, ny)
    ]
    eigs += [remote(ezall.at[c], ezall.at[c], s_eig.at[0], r_eig.at[0], gz=other)]

    def line(buffer, ss, rs, zs, up, index):
        ref = buffer.at[(zs,) + index]
        return remote(ref, ref, ss.at[zs, 0 if up else 1], rs.at[zs], gy=jnp.clip(z + (1 if up else -1), 0, ny - 1))

    def bx_line(zs, up):
        return line(bxb, s_bxz, r_bxz, zs, up, (c,))

    def by_full(zs, t):
        ref = byb.at[zs, p ^ t]
        return remote(ref, ref, s_byf.at[zs, t], r_byf.at[zs, t], gy=jnp.where(low, z + 1, z - 1))

    def by_cross(zs):
        ref = byb.at[zs, p]
        return remote(ref, ref, s_byc.at[zs], r_byc.at[zs], gy=jnp.where(low, mid, mid - 1))

    def across(j):
        return jnp.where(low, mid + j, mid - 1 - j)

    def outside(j):
        return jnp.where(low, z - 1 - j, z + 1 + j)

    def is_outside(j):
        return jnp.where(low, z - 1 - j >= 0, z + 1 + j < ny)

    def goes_on(up):
        return z + 1 < ny if up else z > 0

    def source(r, up):
        zs = z - r if up else z + r
        return zs, jnp.logical_and(zs >= 0, zs < ny)

    def bx_pass(zs):
        return remote(bxb.at[zs, c], bxb.at[zs, c], s_bxd.at[zs], r_bxd.at[zs], gz=other)

    def piece(zs, owner, part):
        return byb.at[zs, owner, pl.ds(part * half, half), :]

    def plane_direct(zs, t):
        slot = 0 if t == 1 else t
        copies = []
        for n, part in enumerate((0, 1) if t == 1 else (1, 0)):
            ref = piece(zs, p, part)
            copies.append(remote(ref, ref, s_byp.at[zs, slot + n], r_byp.at[zs, t, part], gx=p ^ t))
        return copies

    def relay_xy(zs, b):
        ref = piece(zs, p ^ 1, 0)
        return remote(ref, ref, s_byp.at[zs, 2 * nb + b - 1], r_byp.at[zs, 2 * b + 1, 0], gx=p ^ (2 * b))

    def relay_yx(zs, b):
        ref = piece(zs, p ^ (2 * b), 1)
        return remote(ref, ref, s_byp.at[zs, 3 * nb + b - 2], r_byp.at[zs, 2 * b + 1, 1], gx=p ^ 1)

    def wait_piece(zs, t, part):
        ref = piece(zs, p ^ t, part)
        remote(ref, ref, s_byp.at[zs, 0], r_byp.at[zs, t, part], gx=p ^ 1).wait_recv()

    def pass_xy(zs):
        wait_piece(zs, 1, 0)
        for b in range(1, nb):
            relay_xy(zs, b).start()

    def pass_yx(zs):
        for b in range(1, nb):
            wait_piece(zs, 2 * b, 1)
            relay_yx(zs, b).start()

    def plane_y(zs):
        for b in range(1, nb):
            for copy in plane_direct(zs, 2 * b):
                copy.start()

    def plane_x(zs):
        for copy in plane_direct(zs, 1):
            copy.start()

    def g_copies(zs):
        return [
            remote(gs.at[zs, py ^ b], grecv.at[zs, b - 1], s_g.at[zs, b - 1], r_g.at[zs, b - 1], gx=p ^ (2 * b))
            for b in range(1, nb)
        ]

    def first(zs):
        bx_pass_in(zs).wait_recv()

        def tile(i):
            cc, n = i // (yb // yq), i % (yb // yq)
            part = contract(bxb[zs, cc], wide[:, cols(n * yq, yq)], (0, 0)).astype(BF16)
            for b in range(nb):
                gs[zs, b, cc, :, cols(n * yq, yq)] = part[b * ib : (b + 1) * ib]

        loop(2 * (yb // yq), tile)
        for copy in g_copies(zs):
            copy.start()

    def bx_pass_in(zs):
        return remote(bxb.at[zs, other], bxb.at[zs, other], s_bxd.at[zs], r_bxd.at[zs], gz=other)

    def home(zs):
        return jnp.where(zs < mid, mid - 1, mid)

    def g_send(zs):
        return remote(gs.at[zs, py], gall.at[z, c, zs % mid], s_ga.at[zs], r_ga.at[z, zs % mid], gy=home(zs))

    def g_pass(zs, core, blk):
        ref = gall.at[zs, core, blk]
        return remote(ref, ref, s_gd.at[zs, blk], r_gd.at[zs, blk], gz=other)

    def collect(zs):
        for copy in g_copies(zs):
            copy.wait_recv()

        def tile(i):
            cc, n = i // (yb // yq), i % (yb // yq)
            lanes = cols(n * yq, yq)
            total = gs[zs, py, cc, :, lanes].astype(F32)
            for b in range(1, nb):
                total = total + grecv[zs, b - 1, cc, :, lanes].astype(F32)

            @pl.when(home(zs) != z)
            def _():
                gs[zs, py, cc, :, lanes] = total.astype(BF16)

            @pl.when(home(zs) == z)
            def _():
                gall[z, c, zs % mid, cc, :, lanes] = total.astype(BF16)

        loop(2 * (yb // yq), tile)

        @pl.when(home(zs) != z)
        def _():
            g_send(zs).start()

        @pl.when(home(zs) == z)
        def _():
            g_pass(z, c, zs % mid).start()

    def both(r, act):
        for up in (True, False):
            zs, valid = source(r, up)

            @pl.when(valid)
            def _(zs=zs, up=up):
                act(zs, up)

    def onward(maker, zs, up):
        @pl.when(goes_on(up))
        def _():
            maker(zs, up).start()

    def each(r, act):
        for up in (True, False):
            zs, valid = source(r, up)
            valid = jnp.logical_and(valid, r >= 0 if up else r > 0)

            @pl.when(valid)
            def _(zs=zs):
                act(zs)

    def bx_step(zs, up):
        bx_line(zs, up).wait_recv()
        onward(bx_line, zs, up)
        bx_pass(zs).start()

    def crossing(j):
        zs = across(j)
        by_cross(zs).wait_recv()
        plane_y(zs)
        plane_x(zs)

    def cross_outside(j):
        def act():
            by_full(outside(j), 0).wait_recv()
            by_cross(outside(j)).start()

        when(is_outside(j), act)

    def inward(j):
        def act():
            for t in range(nx):
                by_full(outside(j), t).wait_recv()
                by_full(outside(j), t).start()

        when(is_outside(j), act)

    def own_y_inward():
        for b in range(1, nb):
            wait_piece(z, 2 * b, 0)
            by_full(z, 2 * b).start()

    def own_x_inward():
        wait_piece(z, 1, 1)
        by_full(z, 1).start()

    def own_rest_inward():
        for b in range(1, nb):
            wait_piece(z, 2 * b + 1, 0)
            wait_piece(z, 2 * b + 1, 1)
            by_full(z, 2 * b + 1).start()

    def far_relays(j):
        pass_yx(across(j))
        pass_xy(across(j))

    def round_of(i):
        r = i + 1
        both(r, bx_step)

        @pl.when(r == 1)
        def _():
            when(works, lambda: loop(mid - 1, cross_outside))
            remote(wide.at[theirs, :], wide.at[theirs, :], s_head.at[1], r_head.at[1], gx=p ^ 1).wait_recv()
            first(z)

        each(r, first)

        @pl.when(r == 2)
        def _():
            pass_xy(z)
            each(0, collect)
            when(rests, own_x_inward)
            each(1, collect)
            when(works, lambda: loop(mid - 1, lambda j: crossing(j + 1)))
            if mid > 2:
                when(rests, lambda: loop(mid - 1, inward))

        @pl.when(r == 3)
        def _():
            when(works, lambda: pass_xy(across(0)))

        @pl.when(r > 2)
        def _():
            each(r - 1, collect)

        @pl.when(r == 3)
        def _():
            when(works, lambda: pass_yx(across(0)))
            when(works, lambda: loop(mid - 1, lambda j: far_relays(j + 1)))

        @pl.when(r == 4)
        def _():
            when(rests, own_rest_inward)

    local[0].wait()
    when(works, lambda: by_cross(z).start())
    when(rests, lambda: by_full(z, 0).start())
    plane_y(z)
    local[1].wait()
    swap_rhs.start()
    plane_x(z)
    for copy in local[2:]:
        copy.wait()
    ezall[c] = jnp.broadcast_to(ez[...], (8, LANES))
    for copy in eigs:
        copy.start()
    remote(bx.at[:, cols(px * ci, ci)], bxb.at[z, c, theirs, :], s_head.at[0], r_head.at[0], gx=p ^ 1).wait_recv()
    both(0, lambda zs, up: onward(bx_line, zs, up))
    bx_pass(z).start()

    @pl.when(works)
    def _():
        crossing(0)

    pass_yx(z)
    when(rests, own_y_inward)
    loop(max(ny, 4), round_of)

    for t in range(1, nx):
        remote(exall.at[p ^ t], exall.at[p ^ t], s_eig.at[t], r_eig.at[t], gx=p ^ t).wait_recv()
    for d in range(1, ny):
        far = (z - d) % ny
        remote(eyall.at[far], eyall.at[far], s_eig.at[nx + d], r_eig.at[nx + d], gy=(z + d) % ny).wait_recv()
    remote(ezall.at[other], ezall.at[other], s_eig.at[0], r_eig.at[0], gz=other).wait_recv()
    for blk in range(mid):
        for cc in range(2):
            start = ((place * mid + blk) * 2 + cc) * cx + px * ci + py * ib
            line_at = start // LANES
            per = xb // LANES
            row = exall[line_at // per, pl.ds(line_at % per, 1), :]
            lane = lax.broadcasted_iota(jnp.int32, (ib, LANES), 1)
            want = lax.broadcasted_iota(jnp.int32, (ib, LANES), 0) + start % LANES
            column = jnp.sum(jnp.where(lane == want, jnp.broadcast_to(row, (ib, LANES)), 0.0), axis=1, keepdims=True)
            for k in range(2):
                dcol[k, pl.ds((blk * 2 + cc) * ib, ib), :] = jnp.broadcast_to(column, (ib, LANES)) + ezall[k, 0:1, :]

    def arrive(i):
        zs, blk = (z + 1 + i // mid) % ny, i % mid
        remote(gall.at[zs, c, blk], gall.at[zs, c, blk], s_ga.at[zs], r_ga.at[zs, blk], gy=zs).wait_recv()
        g_pass(zs, c, blk).start()

    def passed(i):
        g_pass(i // mid, other, i % mid).wait_recv()

    @pl.when(works)
    def _():
        loop((ny - 1) * mid, arrive)
        loop(ny * mid, passed)

    eacc[...] = jnp.zeros_like(eacc)

    tn = min(cy, 256)
    ni = 2 * mid * ib

    def second(t):
        owner = p ^ t

        def landed(zs):
            outer = jnp.logical_and((zs < mid) == low, zs != z)

            @pl.when(jnp.logical_and(outer, t > 0))
            def _():
                by_full(zs, t).wait_recv()

            @pl.when(jnp.logical_and(jnp.logical_not(outer), t % 2 == 1))
            def _():
                wait_piece(zs, t, 1)

            @pl.when(jnp.logical_and(jnp.logical_not(outer), t > 1))
            def _():
                wait_piece(zs, t, 0)

        loop(ny, landed)

        def tile(i):
            n, k = i // 2, i % 2
            h = None
            for zs in range(ny):
                term = contract(gall[zs, k].reshape(ni, yb), byb[zs, owner, :, cols(n * tn, tn)], (1, 0))
                h = term if h is None else h + term
            for l in range(tn // LANES):
                line_at = ((owner * 2 + c) * cy + n * tn) // LANES + l
                per = yb // LANES
                row = eyall[line_at // per, pl.ds(line_at % per, 1), :]
                part = h[:, l * LANES : (l + 1) * LANES]
                w = part / (dcol[k] + row)
                eacc[...] += jnp.sum((part * w).reshape(-1, 8, LANES), axis=0)
                wbuf[owner, k, :, cols(n * tn + l * LANES, LANES)] = w.astype(BF16)

        loop(2 * (cy // tn), tile)

    when(works, lambda: loop(nx, second))

    def v_pass(q, zs, core):
        lanes = cols(q * yq, yq)
        return remote(
            gall.at[zs, core, :, :, :, lanes], vrecv.at[zs, :, :, :, lanes], s_vd.at[q, zs], r_vd.at[q, zs], gz=other
        )

    def v_slot(q, side, owner):
        return vfull.at[q, pl.ds(side * mid, mid), :, pl.ds(pl.multiple_of(owner * ib, ib), ib), :]

    def v_send(q, zs):
        return remote(
            gall.at[zs, c, :, :, :, cols(q * yq, yq)], v_slot(q, place, py), s_va.at[q, zs], r_va.at[q, place], gy=zs
        )

    def v_copies(q, side):
        slot = v_slot(q, side, py)
        return [
            remote(slot, slot, s_vb.at[q, side, b - 1], r_vb.at[q, side, b - 1], gx=p ^ (2 * b)) for b in range(1, nb)
        ]

    def target_of(d):
        end = jnp.where(d % 2 == 0, ny - 1 - d // 2, d // 2)
        return jnp.where(low, end, ny - 1 - end)

    def third(q, d):
        zs = target_of(d)

        def mode(i):
            k = jnp.where(i == 0, other, c)
            v = None
            for owner in range(nx):
                term = contract(wbuf[owner, k], byb[zs, owner, rows(q * yq, yq), :], (1, 1))
                v = term if v is None else v + term
            gall[zs, k, :, :, :, cols(q * yq, yq)] = v.astype(BF16).reshape(mid, 2, ib, yq)
            when(i == 0, lambda: v_pass(q, zs, other).start())

        loop(2, mode)

    def merge(q, d):
        zs = target_of(d)
        lanes = cols(q * yq, yq)
        v_pass(q, zs, c).wait_recv()
        v = (gall[zs, c, :, :, :, lanes].astype(F32) + vrecv[zs, :, :, :, lanes].astype(F32)).astype(BF16)

        @pl.when(zs != z)
        def _():
            gall[zs, c, :, :, :, lanes] = v
            v_send(q, zs).start()

        @pl.when(zs == z)
        def _():
            vfull[q, pl.ds(place * mid, mid), :, pl.ds(pl.multiple_of(py * ib, ib), ib), :] = v
            for copy in v_copies(q, place):
                copy.start()

    def spread(q):
        def target(i):
            side = jnp.where(low, i, 1 - i)

            @pl.when(mid - 1 + side != z)
            def _():
                slot = v_slot(q, side, py)
                remote(slot, slot, s_va.at[q, 0], r_va.at[q, side], gy=(z + 1) % ny).wait_recv()
                for copy in v_copies(q, side):
                    copy.start()

        loop(2, target)

    mt = min(xb, 512)

    def s_copy(q):
        lanes = cols(q * yq, yq)
        return remote(wide.at[theirs, lanes], srecv.at[:, lanes], s_s.at[q], r_s.at[q], gx=p ^ 1)

    def fourth(q):
        lanes = cols(q * yq, yq)

        def landed(side):
            for b in range(1, nb):
                slot = v_slot(q, side, py ^ b)
                remote(slot, slot, s_vb.at[q, side, b - 1], r_vb.at[q, side, b - 1], gx=p ^ (2 * b)).wait_recv()

        loop(2, landed)

        def tile(i):
            m, own = i % (xb // mt), i // (xb // mt)
            side = jnp.where(own == 1, px, 1 - px)
            at = rows(side * xb + m * mt, mt)
            s = None
            for zs in range(ny):
                for cc in range(2):
                    term = contract(bxb[zs, cc, at, :], vfull[q, zs, cc], (1, 0))
                    s = term if s is None else s + term

            @pl.when(own == 0)
            def _():
                wide[at, lanes] = s.astype(BF16)

                @pl.when(m == xb // mt - 1)
                def _():
                    s_copy(q).start()

            @pl.when(own == 1)
            def _():
                sown[rows(m * mt, mt), lanes] = s

        loop(2 * (xb // mt), tile)

    def out_copy(q):
        lanes = cols(q * yq, yq)
        return pltpu.make_async_copy(wide.at[mine, lanes], out.at[0, :, lanes], s_out.at[q])

    def finish(q):
        lanes = cols(q * yq, yq)
        s_copy(q).wait_recv()

        def tile(m):
            at = rows(m * mt, mt)
            wide[rows(px * xb + m * mt, mt), lanes] = (sown[at, lanes] + srecv[at, lanes].astype(F32)).astype(BF16)

        loop(xb // mt, tile)
        out_copy(q).start()

    def left(i):
        g_pass(i // mid, c, i % mid).wait_send()

    when(works, lambda: loop(ny * mid, left))
    swap_rhs.wait_send()

    e_core = remote(eacc, e1, s_e.at[0], r_e.at[0], gz=other)
    e_plane = [remote(e2.at[p], e2.at[p], s_e.at[t], r_e.at[t], gx=p ^ t) for t in range(1, nx)]
    e_line = [remote(e3.at[place], e3.at[place], s_e.at[nx + d], r_e.at[nx + place], gy=(z + d) % ny) for d in range(1, ny)]

    def leave(q):
        def step(d):
            start = q == 0

            @pl.when(jnp.logical_and(start, d == 0))
            def _():
                e_core.start()

            @pl.when(jnp.logical_and(start, d == 2))
            def _():
                e_core.wait_recv()
                e2[p] = eacc[...] + e1[...]
                for copy in e_plane:
                    copy.start()

            @pl.when(jnp.logical_and(start, d == ny + 1))
            def _():
                for s in range(1, nx):
                    remote(e2.at[p ^ s], e2.at[p ^ s], s_e.at[s], r_e.at[s], gx=p ^ s).wait_recv()
                total = e2[0]
                for s in range(1, nx):
                    total = total + e2[s]
                e3[place] = total
                for copy in e_line:
                    copy.start()

            @pl.when(d < ny)
            def _():
                third(q, d)

            @pl.when(d >= 2)
            def _():
                merge(q, d - 2)

        loop(ny + 2, step)

    def stage(t, lag, act):
        @pl.when(jnp.logical_and(t >= lag, t < chunks + lag))
        def _():
            act(t - lag)

    def tail(t):
        stage(t, 0, lambda q: when(works, lambda: leave(q)))
        stage(t, 1, spread)
        stage(t, 2, fourth)
        stage(t, 3, finish)

    loop(chunks + 3, tail)

    for side in range(2):
        @pl.when(mid - 1 + side != z)
        def _(side=side):
            remote(e3.at[side], e3.at[side], s_e.at[0], r_e.at[nx + side], gy=(z + 1) % ny).wait_recv()

    total = e3[0] + e3[1]
    energy[0] = jnp.sum(total)

    swap_bx.wait_send()
    for copy in eigs:
        copy.wait_send()

    @pl.when(works)
    def _():
        for copy in [e_core] + e_plane + e_line:
            copy.wait_send()

    def plane_drain(zs):
        for t in [1] + [2 * b for b in range(1, nb)]:
            for copy in plane_direct(zs, t):
                copy.wait_send()
        for b in range(1, nb):
            relay_xy(zs, b).wait_send()
            relay_yx(zs, b).wait_send()

    def drain(zs):
        for up in (True, False):
            from_here = zs <= z if up else zs >= z

            @pl.when(jnp.logical_and(goes_on(up), from_here))
            def _(up=up):
                bx_line(zs, up).wait_send()

        bx_pass(zs).wait_send()
        for copy in g_copies(zs):
            copy.wait_send()
        same = (zs < mid) == low
        when(jnp.logical_or(zs == z, jnp.logical_and(works, jnp.logical_not(same))), lambda: plane_drain(zs))
        when(jnp.logical_and(works, same), lambda: by_cross(zs).wait_send())

        @pl.when(jnp.logical_and(jnp.logical_and(jnp.logical_not(works), same), jnp.where(low, zs <= z, zs >= z)))
        def _():
            for t in range(nx):
                by_full(zs, t).wait_send()

        when(home(zs) != z, lambda: g_send(zs).wait_send())

        @pl.when(works)
        def _():
            def chunk(q):
                v_pass(q, zs, other).wait_send()
                when(zs != z, lambda: v_send(q, zs).wait_send())

            loop(chunks, chunk)

    loop(ny, drain)

    def drain_chunk(q):
        s_copy(q).wait_send()
        out_copy(q).wait()
        for side in range(2):
            for copy in v_copies(q, side):
                copy.wait_send()

    loop(chunks, drain_chunk)


def shards(nx, ny, rhs, basis_x, basis_y, eig_x, eig_y, eig_z):
    xb, yb = rhs.shape[1], rhs.shape[2]
    cx, cy = basis_x.shape[1], basis_y.shape[1]
    nb, ci = nx // 2, cx // 2
    ib = ci // nb
    yq = min(yb, 256)
    chunks, mid = yb // yq, ny // 2
    ex = eig_x.reshape(xb // LANES, LANES)
    ey = eig_y.reshape(yb // LANES, LANES)
    ez = eig_z.reshape(1, 1)
    dma = pltpu.SemaphoreType.DMA
    any_space, vmem = pl.BlockSpec(memory_space=pl.ANY), pl.BlockSpec(memory_space=pltpu.VMEM)
    solution, energy = pl.pallas_call(
        functools.partial(kernel, nx, ny, yq),
        name="solve",
        out_shape=(
            jax.ShapeDtypeStruct(rhs.shape, BF16),
            jax.ShapeDtypeStruct((1,), F32),
        ),
        in_specs=[any_space] * 3 + [vmem] * 3,
        out_specs=(any_space, pl.BlockSpec(memory_space=pltpu.SMEM)),
        scratch_shapes=[
            pltpu.VMEM((ny, 2, 2 * xb, ci), BF16),
            pltpu.VMEM((ny, nx, yb, cy), BF16),
            pltpu.VMEM((2 * xb, yb), BF16),
            pltpu.VMEM((ny, nb, 2, ib, yb), BF16),
            pltpu.VMEM((ny, nb - 1, 2, ib, yb), BF16),
            pltpu.VMEM((ny, 2, mid, 2, ib, yb), BF16),
            pltpu.VMEM((nx, 2, 2 * mid * ib, cy), BF16),
            pltpu.VMEM((ny, mid, 2, ib, yb), BF16),
            pltpu.VMEM((chunks, ny, 2, nb * ib, yq), BF16),
            pltpu.VMEM((xb, yb), F32),
            pltpu.VMEM((xb, yb), BF16),
            pltpu.VMEM((nx, xb // LANES, LANES), F32),
            pltpu.VMEM((ny, yb // LANES, LANES), F32),
            pltpu.VMEM((2, 8, LANES), F32),
            pltpu.VMEM((2, 2 * mid * ib, LANES), F32),
            pltpu.VMEM((8, LANES), F32),
            pltpu.VMEM((8, LANES), F32),
            pltpu.VMEM((nx, 8, LANES), F32),
            pltpu.VMEM((2, 8, LANES), F32),
            dma((5,)),
            dma((nx + ny,)), dma((nx + ny,)),
            dma((2,)), dma((2,)),
            dma((ny, 2)), dma((ny,)),
            dma((ny,)), dma((ny,)),
            dma((ny, nx)), dma((ny, nx)),
            dma((ny,)), dma((ny,)),
            dma((ny, 4 * nb - 2)), dma((ny, nx, 2)),
            dma((ny, nb - 1)), dma((ny, nb - 1)),
            dma((ny,)), dma((ny, mid)),
            dma((ny, mid)), dma((ny, mid)),
            dma((chunks, ny)), dma((chunks, ny)),
            dma((chunks, ny)), dma((chunks, 2)),
            dma((chunks, 2, nb - 1)), dma((chunks, 2, nb - 1)),
            dma((chunks,)), dma((chunks,)),
            dma((chunks,)),
            dma((nx + ny,)), dma((nx + ny,)),
        ],
        compiler_params=pltpu.CompilerParams(
            collective_id=0, has_side_effects=True, vmem_limit_bytes=65472 * 1024
        ),
    )(rhs, basis_x, basis_y, ex, ey, ez)
    return solution, energy.reshape(())


def solution(mesh):
    return jax.shard_map(
        functools.partial(shards, mesh.shape["gx"], mesh.shape["gy"]),
        mesh=mesh,
        in_specs=(
            P("gz", "gx", "gy"),
            P("gx", ("gy", "gz")),
            P("gy", ("gx", "gz")),
            P("gx"),
            P("gy"),
            P("gz"),
        ),
        out_specs=(P("gz", "gx", "gy"), P()),
        check_vma=False,
    )
```

time: 322 us -> 271 us (0.84); the launches traced: 316 us -> 271 us
  Pallas kernels: 310 us -> 265 us
    pallas_call x1, Pallas kernels: 310 us -> 265 us  [shards(): pl.pallas_call(functools.partial(kernel, nx, ny, yq), name='solve', out_s...]
where the time goes in v1:
time: 271 us
  Pallas kernels  265 us (98%)
  local copies, waits for them, and re-layouts  3.08 us (1%)
  between operations  3.02 us (1%)
    pallas_call x1, Pallas kernels, shards(): pl.pallas_call(functools.partial(kernel, nx, ny, yq), name='solve', out_s...  265 us

profile of v1, /device:TPU:0, one launch (start us, length us, event | category | flops | bytes accessed | tf_op | source)
XLA Modules:
  0.0 270.6 jit_solution(11655546710767041729)
XLA Ops:
  1.3 264.5 %solve.1 = (bf16[1,1024,1024]{2,1,0:T(8,128)(2,1)}, f32[1]{0:T(128)}) custom-call(bf16[1,1024,1024]{2,1,0:T(8,128)(2,1)} %rhs.1, bf16[1024,512]{1,0:T(8,128)(2,1)} %bx.1, bf16[1024,512]{1,0:T(8,128)(2,1)} %by.1, f32[8,128]{1,0:T(8,128)} %bitcast.5, f32[8,128]{1,0:T(8,128)} %bitcast.6, f32[1,1]{1,0:T(1,128)} %bitcast.4.ez), custom_call_target="tpu_custom_call" | custom-call | tf_op jit(solution)/shard_map/solve/pallas_call | solution.py:695
  265.8 3.1 %copy.11 = bf16[1,1024,1024]{2,1,0:T(8,128)(2,1)} copy(bf16[1,1024,1024]{2,1,0:T(8,128)(2,1)} %get-tuple-element.8) | data formatting | bytes 4194304

commit v2 on v1

--- a/solution.py
+++ b/solution.py
@@ -82,7 +82,12 @@
 
     swap_bx = remote(bx.at[:, cols((1 - px) * ci, ci)], bxb.at[z, c, mine, :], s_head.at[0], r_head.at[0], gx=p ^ 1)
     swap_bx.start()
-    swap_rhs = remote(wide.at[mine, :], wide.at[mine, :], s_head.at[1], r_head.at[1], gx=p ^ 1)
+    wing = yb // 2
+
+    def swap_rhs(side, part):
+        ref = wide.at[side, pl.ds(part * wing, wing)]
+        return remote(ref, ref, s_head.at[1 + part], r_head.at[1 + part], gx=p ^ 1)
+
     eigs = [remote(exall.at[p], exall.at[p], s_eig.at[t], r_eig.at[t], gx=p ^ t) for t in range(1, nx)]
     eigs += [
         remote(eyall.at[z], eyall.at[z], s_eig.at[nx + d], r_eig.at[nx + d], gy=(z + d) % ny) for d in range(1, ny)
@@ -96,9 +101,11 @@
     def bx_line(zs, up):
         return line(bxb, s_bxz, r_bxz, zs, up, (c,))
 
-    def by_full(zs, t):
-        ref = byb.at[zs, p ^ t]
-        return remote(ref, ref, s_byf.at[zs, t], r_byf.at[zs, t], gy=jnp.where(low, z + 1, z - 1))
+    def by_full(zs, t, part):
+        ref = piece(zs, p ^ t, part)
+        return remote(
+            ref, ref, s_byf.at[zs, t, part], r_byf.at[zs, t, part], gy=jnp.where(low, z + 1, z - 1)
+        )
 
     def by_cross(zs):
         ref = byb.at[zs, p]
@@ -165,24 +172,39 @@
         for copy in plane_direct(zs, 1):
             copy.start()
 
-    def g_copies(zs):
+    def g_copies(zs, part):
+        lanes = pl.ds(part * wing, wing)
         return [
-            remote(gs.at[zs, py ^ b], grecv.at[zs, b - 1], s_g.at[zs, b - 1], r_g.at[zs, b - 1], gx=p ^ (2 * b))
+            remote(
+                gs.at[zs, py ^ b, :, :, lanes], grecv.at[zs, b - 1, :, :, lanes],
+                s_g.at[zs, part, b - 1], r_g.at[zs, part, b - 1], gx=p ^ (2 * b),
+            )
             for b in range(1, nb)
         ]
 
-    def first(zs):
+    def first(zs, part):
+        def tile(i):
+            cc, n = i // (wing // yq), i % (wing // yq)
+            lanes = cols(part * wing + n * yq, yq)
+            sums = contract(bxb[zs, cc], wide[:, lanes], (0, 0)).astype(BF16)
+            for b in range(nb):
+                gs[zs, b, cc, :, lanes] = sums[b * ib : (b + 1) * ib]
+
+        loop(2 * (wing // yq), tile)
+        for copy in g_copies(zs, part):
+            copy.start()
+
+    def first_whole(zs):
         bx_pass_in(zs).wait_recv()
-
-        def tile(i):
-            cc, n = i // (yb // yq), i % (yb // yq)
-            part = contract(bxb[zs, cc], wide[:, cols(n * yq, yq)], (0, 0)).astype(BF16)
-            for b in range(nb):
-                gs[zs, b, cc, :, cols(n * yq, yq)] = part[b * ib : (b + 1) * ib]
-
-        loop(2 * (yb // yq), tile)
-        for copy in g_copies(zs):
-            copy.start()
+        first(zs, 0)
+        first(zs, 1)
+
+    def first_left(zs):
+        bx_pass_in(zs).wait_recv()
+        first(zs, 0)
+
+    def first_right(zs):
+        first(zs, 1)
 
     def bx_pass_in(zs):
         return remote(bxb.at[zs, other], bxb.at[zs, other], s_bxd.at[zs], r_bxd.at[zs], gz=other)
@@ -198,8 +220,9 @@
         return remote(ref, ref, s_gd.at[zs, blk], r_gd.at[zs, blk], gz=other)
 
     def collect(zs):
-        for copy in g_copies(zs):
-            copy.wait_recv()
+        for part in range(2):
+            for copy in g_copies(zs, part):
+                copy.wait_recv()
 
         def tile(i):
             cc, n = i // (yb // yq), i % (yb // yq)
@@ -261,7 +284,8 @@
 
     def cross_outside(j):
         def act():
-            by_full(outside(j), 0).wait_recv()
+            for part in range(2):
+                by_full(outside(j), 0, part).wait_recv()
             by_cross(outside(j)).start()
 
         when(is_outside(j), act)
@@ -269,25 +293,27 @@
     def inward(j):
         def act():
             for t in range(nx):
-                by_full(outside(j), t).wait_recv()
-                by_full(outside(j), t).start()
+                for part in range(2):
+                    by_full(outside(j), t, part).wait_recv()
+                    by_full(outside(j), t, part).start()
 
         when(is_outside(j), act)
 
     def own_y_inward():
         for b in range(1, nb):
+            by_full(z, 2 * b, 1).start()
             wait_piece(z, 2 * b, 0)
-            by_full(z, 2 * b).start()
+            by_full(z, 2 * b, 0).start()
 
     def own_x_inward():
         wait_piece(z, 1, 1)
-        by_full(z, 1).start()
+        by_full(z, 1, 1).start()
 
     def own_rest_inward():
         for b in range(1, nb):
-            wait_piece(z, 2 * b + 1, 0)
-            wait_piece(z, 2 * b + 1, 1)
-            by_full(z, 2 * b + 1).start()
+            for part in range(2):
+                wait_piece(z, 2 * b + 1, part)
+                by_full(z, 2 * b + 1, part).start()
 
     def far_relays(j):
         pass_yx(across(j))
@@ -300,16 +326,23 @@
         @pl.when(r == 1)
         def _():
             when(works, lambda: loop(mid - 1, cross_outside))
-            remote(wide.at[theirs, :], wide.at[theirs, :], s_head.at[1], r_head.at[1], gx=p ^ 1).wait_recv()
-            first(z)
-
-        each(r, first)
+            each(1, first_left)
+            swap_rhs(theirs, 1).wait_recv()
+            first(z, 1)
+            each(1, first_right)
 
         @pl.when(r == 2)
         def _():
             pass_xy(z)
+            when(rests, lambda: by_full(z, 1, 0).start())
+
+        @pl.when(r > 1)
+        def _():
+            each(r, first_whole)
+
+        @pl.when(r == 2)
+        def _():
             each(0, collect)
-            when(rests, own_x_inward)
             each(1, collect)
             when(works, lambda: loop(mid - 1, lambda j: crossing(j + 1)))
             if mid > 2:
@@ -330,14 +363,17 @@
 
         @pl.when(r == 4)
         def _():
+            when(rests, own_x_inward)
             when(rests, own_rest_inward)
 
     local[0].wait()
     when(works, lambda: by_cross(z).start())
-    when(rests, lambda: by_full(z, 0).start())
+    for part in range(2):
+        when(rests, lambda part=part: by_full(z, 0, part).start())
     plane_y(z)
     local[1].wait()
-    swap_rhs.start()
+    swap_rhs(mine, 0).start()
+    swap_rhs(mine, 1).start()
     plane_x(z)
     for copy in local[2:]:
         copy.wait()
@@ -354,6 +390,8 @@
 
     pass_yx(z)
     when(rests, own_y_inward)
+    swap_rhs(theirs, 0).wait_recv()
+    first_left(z)
     loop(max(ny, 4), round_of)
 
     for t in range(1, nx):
@@ -400,7 +438,8 @@
 
             @pl.when(jnp.logical_and(outer, t > 0))
             def _():
-                by_full(zs, t).wait_recv()
+                for part in range(2):
+                    by_full(zs, t, part).wait_recv()
 
             @pl.when(jnp.logical_and(jnp.logical_not(outer), t % 2 == 1))
             def _():
@@ -558,7 +597,8 @@
         g_pass(i // mid, c, i % mid).wait_send()
 
     when(works, lambda: loop(ny * mid, left))
-    swap_rhs.wait_send()
+    swap_rhs(mine, 0).wait_send()
+    swap_rhs(mine, 1).wait_send()
 
     e_core = remote(eacc, e1, s_e.at[0], r_e.at[0], gz=other)
     e_plane = [remote(e2.at[p], e2.at[p], s_e.at[t], r_e.at[t], gx=p ^ t) for t in range(1, nx)]
@@ -594,7 +634,7 @@
             def _():
                 third(q, d)
 
-            @pl.when(d >= 2)
+            @pl.when(jnp.logical_and(start, d >= 2))
             def _():
                 merge(q, d - 2)
 
@@ -608,6 +648,11 @@
     def tail(t):
         stage(t, 0, lambda q: when(works, lambda: leave(q)))
         stage(t, 1, spread)
+
+        @pl.when(jnp.logical_and(works, jnp.logical_and(t >= 1, t < chunks)))
+        def _():
+            loop(ny, lambda d: merge(t, d))
+
         stage(t, 2, fourth)
         stage(t, 3, finish)
 
@@ -647,8 +692,9 @@
                 bx_line(zs, up).wait_send()
 
         bx_pass(zs).wait_send()
-        for copy in g_copies(zs):
-            copy.wait_send()
+        for part in range(2):
+            for copy in g_copies(zs, part):
+                copy.wait_send()
         same = (zs < mid) == low
         when(jnp.logical_or(zs == z, jnp.logical_and(works, jnp.logical_not(same))), lambda: plane_drain(zs))
         when(jnp.logical_and(works, same), lambda: by_cross(zs).wait_send())
@@ -656,7 +702,8 @@
         @pl.when(jnp.logical_and(jnp.logical_and(jnp.logical_not(works), same), jnp.where(low, zs <= z, zs >= z)))
         def _():
             for t in range(nx):
-                by_full(zs, t).wait_send()
+                for part in range(2):
+                    by_full(zs, t, part).wait_send()
 
         when(home(zs) != z, lambda: g_send(zs).wait_send())
 
@@ -723,13 +770,13 @@
             pltpu.VMEM((2, 8, LANES), F32),
             dma((5,)),
             dma((nx + ny,)), dma((nx + ny,)),
-            dma((2,)), dma((2,)),
+            dma((3,)), dma((3,)),
             dma((ny, 2)), dma((ny,)),
             dma((ny,)), dma((ny,)),
-            dma((ny, nx)), dma((ny, nx)),
+            dma((ny, nx, 2)), dma((ny, nx, 2)),
             dma((ny,)), dma((ny,)),
             dma((ny, 4 * nb - 2)), dma((ny, nx, 2)),
-            dma((ny, nb - 1)), dma((ny, nb - 1)),
+            dma((ny, 2, nb - 1)), dma((ny, 2, nb - 1)),
             dma((ny,)), dma((ny, mid)),
             dma((ny, mid)), dma((ny, mid)),
             dma((chunks, ny)), dma((chunks, ny)),

time: 271 us -> 259 us (0.956)
  Pallas kernels: 265 us -> 253 us
    pallas_call x1, Pallas kernels: 265 us -> 253 us  [shards(): pl.pallas_call(functools.partial(kernel, nx, ny, yq), name='solve', out_s...]
where the time goes in v2:
time: 259 us
  Pallas kernels  253 us (98%)
  local copies, waits for them, and re-layouts  3.08 us (1%)
  between operations  3.02 us (1%)
    pallas_call x1, Pallas kernels, shards(): pl.pallas_call(functools.partial(kernel, nx, ny, yq), name='solve', out_s...  253 us

profile of v2, /device:TPU:0, one launch (start us, length us, event | category | flops | bytes accessed | tf_op | source)
XLA Modules:
  0.0 259.0 jit_solution(17193782020472175412)
XLA Ops:
  1.3 252.9 %solve.1 = (bf16[1,1024,1024]{2,1,0:T(8,128)(2,1)}, f32[1]{0:T(128)}) custom-call(bf16[1,1024,1024]{2,1,0:T(8,128)(2,1)} %rhs.1, bf16[1024,512]{1,0:T(8,128)(2,1)} %bx.1, bf16[1024,512]{1,0:T(8,128)(2,1)} %by.1, f32[8,128]{1,0:T(8,128)} %bitcast.5, f32[8,128]{1,0:T(8,128)} %bitcast.6, f32[1,1]{1,0:T(1,128)} %bitcast.4.ez), custom_call_target="tpu_custom_call" | custom-call | tf_op jit(solution)/shard_map/solve/pallas_call | solution.py:742
  254.2 3.1 %copy.11 = bf16[1,1024,1024]{2,1,0:T(8,128)(2,1)} copy(bf16[1,1024,1024]{2,1,0:T(8,128)(2,1)} %get-tuple-element.8) | data formatting | bytes 4194304

commit v3 on v2

--- a/solution.py
+++ b/solution.py
@@ -104,12 +104,12 @@
     def by_full(zs, t, part):
         ref = piece(zs, p ^ t, part)
         return remote(
-            ref, ref, s_byf.at[zs, t, part], r_byf.at[zs, t, part], gy=jnp.where(low, z + 1, z - 1)
+            ref, ref, s_byf.at[zs % mid, t, part], r_byf.at[zs % mid, t, part], gy=jnp.where(low, z + 1, z - 1)
         )
 
     def by_cross(zs):
         ref = byb.at[zs, p]
-        return remote(ref, ref, s_byc.at[zs], r_byc.at[zs], gy=jnp.where(low, mid, mid - 1))
+        return remote(ref, ref, s_byc.at[zs % mid], r_byc.at[zs % mid], gy=jnp.where(low, mid, mid - 1))
 
     def across(j):
         return jnp.where(low, mid + j, mid - 1 - j)
@@ -133,25 +133,27 @@
     def piece(zs, owner, part):
         return byb.at[zs, owner, pl.ds(part * half, half), :]
 
+    def row_of(zs):
+        return jnp.where(zs == z, 0, 1 + zs % mid)
+
     def plane_direct(zs, t):
-        slot = 0 if t == 1 else t
         copies = []
-        for n, part in enumerate((0, 1) if t == 1 else (1, 0)):
+        for part in (0, 1) if t == 1 else (1, 0):
             ref = piece(zs, p, part)
-            copies.append(remote(ref, ref, s_byp.at[zs, slot + n], r_byp.at[zs, t, part], gx=p ^ t))
+            copies.append(remote(ref, ref, s_byp.at[row_of(zs)], r_byp.at[row_of(zs), t - 1, part], gx=p ^ t))
         return copies
 
     def relay_xy(zs, b):
         ref = piece(zs, p ^ 1, 0)
-        return remote(ref, ref, s_byp.at[zs, 2 * nb + b - 1], r_byp.at[zs, 2 * b + 1, 0], gx=p ^ (2 * b))
+        return remote(ref, ref, s_byp.at[row_of(zs)], r_byp.at[row_of(zs), 2 * b, 0], gx=p ^ (2 * b))
 
     def relay_yx(zs, b):
         ref = piece(zs, p ^ (2 * b), 1)
-        return remote(ref, ref, s_byp.at[zs, 3 * nb + b - 2], r_byp.at[zs, 2 * b + 1, 1], gx=p ^ 1)
+        return remote(ref, ref, s_byp.at[row_of(zs)], r_byp.at[row_of(zs), 2 * b, 1], gx=p ^ 1)
 
     def wait_piece(zs, t, part):
         ref = piece(zs, p ^ t, part)
-        remote(ref, ref, s_byp.at[zs, 0], r_byp.at[zs, t, part], gx=p ^ 1).wait_recv()
+        remote(ref, ref, s_byp.at[row_of(zs)], r_byp.at[row_of(zs), t - 1, part], gx=p ^ 1).wait_recv()
 
     def pass_xy(zs):
         wait_piece(zs, 1, 0)
@@ -217,7 +219,7 @@
 
     def g_pass(zs, core, blk):
         ref = gall.at[zs, core, blk]
-        return remote(ref, ref, s_gd.at[zs, blk], r_gd.at[zs, blk], gz=other)
+        return remote(ref, ref, s_gd, r_gd.at[zs, blk], gz=other)
 
     def collect(zs):
         for part in range(2):
@@ -473,7 +475,7 @@
     def v_pass(q, zs, core):
         lanes = cols(q * yq, yq)
         return remote(
-            gall.at[zs, core, :, :, :, lanes], vrecv.at[zs, :, :, :, lanes], s_vd.at[q, zs], r_vd.at[q, zs], gz=other
+            gall.at[zs, core, :, :, :, lanes], vrecv.at[zs, :, :, :, lanes], s_vd.at[q], r_vd.at[q, zs], gz=other
         )
 
     def v_slot(q, side, owner):
@@ -481,7 +483,7 @@
 
     def v_send(q, zs):
         return remote(
-            gall.at[zs, c, :, :, :, cols(q * yq, yq)], v_slot(q, place, py), s_va.at[q, zs], r_va.at[q, place], gy=zs
+            gall.at[zs, c, :, :, :, cols(q * yq, yq)], v_slot(q, place, py), s_va.at[q], r_va.at[q, place], gy=zs
         )
 
     def v_copies(q, side):
@@ -532,7 +534,7 @@
             @pl.when(mid - 1 + side != z)
             def _():
                 slot = v_slot(q, side, py)
-                remote(slot, slot, s_va.at[q, 0], r_va.at[q, side], gy=(z + 1) % ny).wait_recv()
+                remote(slot, slot, s_va.at[q], r_va.at[q, side], gy=(z + 1) % ny).wait_recv()
                 for copy in v_copies(q, side):
                     copy.start()
 
@@ -540,9 +542,12 @@
 
     mt = min(xb, 512)
 
-    def s_copy(q):
+    def s_copy(q, m):
         lanes = cols(q * yq, yq)
-        return remote(wide.at[theirs, lanes], srecv.at[:, lanes], s_s.at[q], r_s.at[q], gx=p ^ 1)
+        return remote(
+            wide.at[rows((1 - px) * xb + m * mt, mt), lanes], srecv.at[rows(m * mt, mt), lanes],
+            s_s.at[q, m], r_s.at[q, m], gx=p ^ 1,
+        )
 
     def fourth(q):
         lanes = cols(q * yq, yq)
@@ -567,10 +572,7 @@
             @pl.when(own == 0)
             def _():
                 wide[at, lanes] = s.astype(BF16)
-
-                @pl.when(m == xb // mt - 1)
-                def _():
-                    s_copy(q).start()
+                s_copy(q, m).start()
 
             @pl.when(own == 1)
             def _():
@@ -578,25 +580,27 @@
 
         loop(2 * (xb // mt), tile)
 
-    def out_copy(q):
+    def out_copy(q, m):
         lanes = cols(q * yq, yq)
-        return pltpu.make_async_copy(wide.at[mine, lanes], out.at[0, :, lanes], s_out.at[q])
+        return pltpu.make_async_copy(
+            wide.at[rows(px * xb + m * mt, mt), lanes], out.at[0, rows(m * mt, mt), lanes], s_out.at[q, m]
+        )
 
     def finish(q):
         lanes = cols(q * yq, yq)
-        s_copy(q).wait_recv()
 
         def tile(m):
             at = rows(m * mt, mt)
+            s_copy(q, m).wait_recv()
             wide[rows(px * xb + m * mt, mt), lanes] = (sown[at, lanes] + srecv[at, lanes].astype(F32)).astype(BF16)
+            out_copy(q, m).start()
 
         loop(xb // mt, tile)
-        out_copy(q).start()
-
-    def left(i):
-        g_pass(i // mid, c, i % mid).wait_send()
-
-    when(works, lambda: loop(ny * mid, left))
+
+    @pl.when(works)
+    def _():
+        remote(gall.at[:, c], gall.at[:, c], s_gd, r_gd.at[0, 0], gz=other).wait_send()
+
     swap_rhs(mine, 0).wait_send()
     swap_rhs(mine, 1).wait_send()
 
@@ -676,12 +680,8 @@
             copy.wait_send()
 
     def plane_drain(zs):
-        for t in [1] + [2 * b for b in range(1, nb)]:
-            for copy in plane_direct(zs, t):
-                copy.wait_send()
-        for b in range(1, nb):
-            relay_xy(zs, b).wait_send()
-            relay_yx(zs, b).wait_send()
+        sent = byb.at[zs, pl.ds(0, 2 * nb - 1)]
+        remote(sent, sent, s_byp.at[row_of(zs)], r_byp.at[0, 0, 0], gx=p ^ 1).wait_send()
 
     def drain(zs):
         for up in (True, False):
@@ -707,22 +707,25 @@
 
         when(home(zs) != z, lambda: g_send(zs).wait_send())
 
+    loop(ny, drain)
+
+    def drain_chunk(q):
         @pl.when(works)
         def _():
-            def chunk(q):
-                v_pass(q, zs, other).wait_send()
-                when(zs != z, lambda: v_send(q, zs).wait_send())
-
-            loop(chunks, chunk)
-
-    loop(ny, drain)
-
-    def drain_chunk(q):
-        s_copy(q).wait_send()
-        out_copy(q).wait()
+            lanes = cols(q * yq, yq)
+            passed_on, sent = vrecv.at[:, :, :, :, lanes], vrecv.at[pl.ds(0, ny - 1), :, :, :, lanes]
+            remote(passed_on, passed_on, s_vd.at[q], r_vd.at[q, 0], gz=other).wait_send()
+            remote(sent, sent, s_va.at[q], r_va.at[q, 0], gy=(z + 1) % ny).wait_send()
+
         for side in range(2):
             for copy in v_copies(q, side):
                 copy.wait_send()
+
+        def tile(m):
+            s_copy(q, m).wait_send()
+            out_copy(q, m).wait()
+
+        loop(xb // mt, tile)
 
     loop(chunks, drain_chunk)
 
@@ -733,7 +736,7 @@
     nb, ci = nx // 2, cx // 2
     ib = ci // nb
     yq = min(yb, 256)
-    chunks, mid = yb // yq, ny // 2
+    chunks, mid, tiles = yb // yq, ny // 2, xb // min(xb, 512)
     ex = eig_x.reshape(xb // LANES, LANES)
     ey = eig_y.reshape(yb // LANES, LANES)
     ez = eig_z.reshape(1, 1)
@@ -773,17 +776,17 @@
             dma((3,)), dma((3,)),
             dma((ny, 2)), dma((ny,)),
             dma((ny,)), dma((ny,)),
-            dma((ny, nx, 2)), dma((ny, nx, 2)),
-            dma((ny,)), dma((ny,)),
-            dma((ny, 4 * nb - 2)), dma((ny, nx, 2)),
+            dma((mid, nx, 2)), dma((mid, nx, 2)),
+            dma((mid,)), dma((mid,)),
+            dma((mid + 1,)), dma((mid + 1, nx - 1, 2)),
             dma((ny, 2, nb - 1)), dma((ny, 2, nb - 1)),
             dma((ny,)), dma((ny, mid)),
-            dma((ny, mid)), dma((ny, mid)),
-            dma((chunks, ny)), dma((chunks, ny)),
-            dma((chunks, ny)), dma((chunks, 2)),
+            pltpu.SemaphoreType.DMA, dma((ny, mid)),
+            dma((chunks,)), dma((chunks, ny)),
+            dma((chunks,)), dma((chunks, 2)),
             dma((chunks, 2, nb - 1)), dma((chunks, 2, nb - 1)),
-            dma((chunks,)), dma((chunks,)),
-            dma((chunks,)),
+            dma((chunks, tiles)), dma((chunks, tiles)),
+            dma((chunks, tiles)),
             dma((nx + ny,)), dma((nx + ny,)),
         ],
         compiler_params=pltpu.CompilerParams(

time: 259 us -> 257 us (level)
  no operation moved by 1% of the time
where the time goes in v3:
time: 257 us
  Pallas kernels  251 us (98%)
  local copies, waits for them, and re-layouts  3.08 us (1%)
  between operations  3.02 us (1%)
    pallas_call x1, Pallas kernels, shards(): pl.pallas_call(functools.partial(kernel, nx, ny, yq), name='solve', out_s...  251 us

profile of v3, /device:TPU:0, one launch (start us, length us, event | category | flops | bytes accessed | tf_op | source)
XLA Modules:
  0.0 257.2 jit_solution(3429210494739389209)
XLA Ops:
  1.3 251.1 %solve.1 = (bf16[1,1024,1024]{2,1,0:T(8,128)(2,1)}, f32[1]{0:T(128)}) custom-call(bf16[1,1024,1024]{2,1,0:T(8,128)(2,1)} %rhs.1, bf16[1024,512]{1,0:T(8,128)(2,1)} %bx.1, bf16[1024,512]{1,0:T(8,128)(2,1)} %by.1, f32[8,128]{1,0:T(8,128)} %bitcast.5, f32[8,128]{1,0:T(8,128)} %bitcast.6, f32[1,1]{1,0:T(1,128)} %bitcast.4.ez), custom_call_target="tpu_custom_call" | custom-call | tf_op jit(solution)/shard_map/solve/pallas_call | solution.py:745
  252.4 3.1 %copy.11 = bf16[1,1024,1024]{2,1,0:T(8,128)(2,1)} copy(bf16[1,1024,1024]{2,1,0:T(8,128)(2,1)} %get-tuple-element.8) | data formatting | bytes 4194304

commit v4 on v3

--- a/solution.py
+++ b/solution.py
@@ -292,9 +292,17 @@
 
         when(is_outside(j), act)
 
+    def inward_first(j):
+        def act():
+            for part in range(2):
+                by_full(outside(j), 0, part).wait_recv()
+                by_full(outside(j), 0, part).start()
+
+        when(is_outside(j), act)
+
     def inward(j):
         def act():
-            for t in range(nx):
+            for t in range(1, nx):
                 for part in range(2):
                     by_full(outside(j), t, part).wait_recv()
                     by_full(outside(j), t, part).start()
@@ -328,6 +336,8 @@
         @pl.when(r == 1)
         def _():
             when(works, lambda: loop(mid - 1, cross_outside))
+            if mid > 2:
+                when(rests, lambda: loop(mid - 1, inward_first))
             each(1, first_left)
             swap_rhs(theirs, 1).wait_recv()
             first(z, 1)
@@ -347,8 +357,6 @@
             each(0, collect)
             each(1, collect)
             when(works, lambda: loop(mid - 1, lambda j: crossing(j + 1)))
-            if mid > 2:
-                when(rests, lambda: loop(mid - 1, inward))
 
         @pl.when(r == 3)
         def _():
@@ -395,6 +403,8 @@
     swap_rhs(theirs, 0).wait_recv()
     first_left(z)
     loop(max(ny, 4), round_of)
+    if mid > 2:
+        when(rests, lambda: loop(mid - 1, inward))
 
     for t in range(1, nx):
         remote(exall.at[p ^ t], exall.at[p ^ t], s_eig.at[t], r_eig.at[t], gx=p ^ t).wait_recv()

time: 257 us -> 257 us (level)
  no operation moved by 1% of the time
where the time goes in v4:
time: 257 us
  Pallas kernels  251 us (98%)
  local copies, waits for them, and re-layouts  3.08 us (1%)
  between operations  3.02 us (1%)
    pallas_call x1, Pallas kernels, shards(): pl.pallas_call(functools.partial(kernel, nx, ny, yq), name='solve', out_s...  251 us

profile of v4, /device:TPU:0, one launch (start us, length us, event | category | flops | bytes accessed | tf_op | source)
XLA Modules:
  0.0 257.2 jit_solution(3429210494739389209)
XLA Ops:
  1.3 251.1 %solve.1 = (bf16[1,1024,1024]{2,1,0:T(8,128)(2,1)}, f32[1]{0:T(128)}) custom-call(bf16[1,1024,1024]{2,1,0:T(8,128)(2,1)} %rhs.1, bf16[1024,512]{1,0:T(8,128)(2,1)} %bx.1, bf16[1024,512]{1,0:T(8,128)(2,1)} %by.1, f32[8,128]{1,0:T(8,128)} %bitcast.5, f32[8,128]{1,0:T(8,128)} %bitcast.6, f32[1,1]{1,0:T(1,128)} %bitcast.4.ez), custom_call_target="tpu_custom_call" | custom-call | tf_op jit(solution)/shard_map/solve/pallas_call | solution.py:755
  252.4 3.1 %copy.11 = bf16[1,1024,1024]{2,1,0:T(8,128)(2,1)} copy(bf16[1,1024,1024]{2,1,0:T(8,128)(2,1)} %get-tuple-element.8) | data formatting | bytes 4194304
